TPU v7x, 256 devices: a whole 4x4x8 slice. The times are simulated.
256 devices in a mesh: gy: 8 (over y, x_hi), gx: 32 (over x_lo, z, core).
Axes of the slice: x: 4 (x_hi: 2, x_lo: 2; x = x_hi * 2 + x_lo), y: 4, z: 8, core: 2. Of those that a mesh axis runs over, the one named last changes fastest.
Arguments:
- u_field: float32 [8, 2048, 2048], P(None, 'gx', 'gy')
- v_field: float32 [8, 2048, 2048], P(None, 'gx', 'gy')
- w_field: float32 [8, 2048, 2048], P(None, 'gx', 'gy')
- sep_x: int32 [16], replicated, may hold values from 1 to 128, as said below
- sep_y: int32 [16], replicated, may hold values from 1 to 256, as said below
- sep_z: int32 [16], replicated, may hold values from 1 to 4
Outputs:
- correlation: float32 [3, 16], replicated
Inputs may be any that keep to these rules, and one draw needn't show every extreme that they name: `sep_x`: every separation along x lies in 1 to 128, and 128 is among them in every draw; repeats may occur. `sep_y`: every separation along y lies in 1 to 256, and 256 is among them in every draw; repeats may occur.
All inputs are finite; a program needn't handle non-finite values.
Results may differ from a plain program's by a relative error of at most 0.0003.
Values sent between devices are 32-bit elements; how exact they have to be, the bound alone decides.
A program may use at most 64 MiB of HBM per device.

v0:
```python
import jax
import jax.numpy as jnp
from jax import lax
from jax.sharding import Mesh
from jax.sharding import PartitionSpec as P

GX = ("gx_0", "gx_1", "gx_2")
GY = ("gy_0", "gy_1")
GY_GX = ("gy_0", "gy_1", "gx_0", "gx_1", "gx_2")


def from_behind(value, axis, steps):
    count = lax.axis_size(axis)
    pairs = [(source, (source + steps) % count) for source in range(count)]
    return lax.ppermute(value, axis, pairs)


def by_axis(x, axes):
    for axis in axes:
        x = lax.psum(x, axis)
    return x


def lag_sums(widened, leading, lag_values, length, axis_dim):

    def one_lag(lag_entry):
        offset, lag_value = lag_entry
        head = lax.dynamic_slice_in_dim(widened, offset, length, axis_dim)
        tail = lax.dynamic_slice_in_dim(widened, offset + lag_value, length, axis_dim)
        return jnp.sum(head * tail)

    return lax.map(one_lag, (leading, lag_values))


def local(u_field, v_field, w_field, sep_x, sep_y, sep_z):
    planes, width_x, width_y = u_field.shape
    u_next = from_behind(u_field, GX, -1)
    u_after = from_behind(u_next, GX, -1)
    wide_x = jnp.concatenate([u_field, u_next, u_after], axis=1)
    v_next = from_behind(v_field, GY, -1)
    wide_y = jnp.concatenate([v_field, v_next], axis=2)
    offset_x = jnp.zeros_like(sep_x)
    offset_y = jnp.zeros_like(sep_y)
    sums_x = lag_sums(wide_x, offset_x, sep_x, width_x, 1)
    sums_y = lag_sums(wide_y, offset_y, sep_y, width_y, 2)
    padded = jnp.concatenate([w_field, jnp.zeros_like(w_field)], axis=0)

    def along_z(lag_value):
        shifted = lax.dynamic_slice_in_dim(padded, lag_value, planes, 0)
        return jnp.sum(w_field * shifted)

    sums_z = lax.map(along_z, sep_z)
    products = jnp.stack([sums_x, sums_y, sums_z], axis=0)
    squares = jnp.stack(
        [jnp.sum(u_field * u_field), jnp.sum(v_field * v_field), jnp.sum(w_field * w_field)]
    )
    totals, energy = (by_axis(products, GY_GX), by_axis(squares, GY_GX))
    factor = jnp.float32(planes) / (jnp.float32(planes) - sep_z.astype(jnp.float32))
    row_x = totals[0] / energy[0]
    row_y = totals[1] / energy[1]
    row_z = totals[2] / energy[2] * factor
    return jnp.stack([row_x, row_y, row_z], axis=0)


def solution(mesh):
    finer = Mesh(mesh.devices.reshape(4, 2, 2, 8, 2), ("gy_0", "gy_1", "gx_0", "gx_1", "gx_2"))
    placed = (P(None, GX, GY), P(None, GX, GY), P(None, GX, GY), P(), P(), P())
    return jax.shard_map(local, mesh=finer, in_specs=placed, out_specs=P(), check_vma=False)
```

profile of v0, /device:TPU:1, one launch (start us, length us, event | category | flops | bytes accessed | tf_op | source)
XLA Modules:
  0.0 266.0 jit_solution(17516855033638149033)
XLA Ops:
  0.0 3.2 %collective-permute-start = (f32[8,64,256]{2,1,0:T(8,128)}, f32[8,64,256]{2,1,0:T(8,128)S(1)}, u32[]{:S(2)}, u32[]{:S(2)}) collective-permute-start(f32[8,64,256]{2,1,0:T(8,128)} %param.12), channel_id=1, source_target_pairs={{0,31},{1,0},{2,1},{3,2},{4,3},{5,4},{6,5},{7,6},{8,7},{9,8},{10,9... | collective-permute-start | bytes 1572872 | tf_op jit(solution)/shard_map/ppermute | solution.py:15
  3.2 3.5 %collective-permute-start.2 = (f32[8,64,256]{2,1,0:T(8,128)}, f32[8,64,256]{2,1,0:T(8,128)}, u32[]{:S(2)}, u32[]{:S(2)}) collective-permute-start(f32[8,64,256]{2,1,0:T(8,128)} %param.13), channel_id=1, source_target_pairs={{0,224},{32,0},{64,32},{96,64},{128,96},{160,128},{192,160},{224,1... | collective-permute-start | bytes 1572872 | tf_op jit(solution)/shard_map/ppermute | solution.py:15
  6.7 1.1 concatenate.11
  7.9 69.8 %while.32 = (s32[]{:T(128)}, f32[16]{0:T(128)S(1)}, s32[16]{0:T(128)S(1)}, f32[16,64,256]{2,1,0:T(8,128)S(1)}, f32[8,64,256]{2,1,0:T(8,128)S(1)}, /*index=5*/s32[]{:T(128)}, s32[]{:T(128)}, s32[]{:T(128)}) while((s32[]{:T(128)}, f32[16]{0:T(128)S(1)}, s32[16]{0:T(128)S(1)}, f32[16,64,256]{2,1,0:T(8,128)S(1)}, f32[8,64,256]{2,1,0:T(8,128)S(1)}, ...), condition=%wide.region_8.9_spmd, body=%wide.region_6.8_spmd.sunk | while | flops 262148 | bytes 1048727 | solution.py:52
  80.1 2.0 pad_maximum_fusion.4
  82.0 6.2 %collective-permute-start.1 = (f32[8,64,256]{2,1,0:T(8,128)S(1)}, f32[8,64,256]{2,1,0:T(8,128)}, u32[]{:S(2)}, u32[]{:S(2)}) collective-permute-start(f32[8,64,256]{2,1,0:T(8,128)S(1)} %collective-permute-done), channel_id=1, source_target_pairs={{0,31},{1,0},{2,1},{3,2},{4,3},{5,4},{6,5},{7,6},{8,7},{9,8},{10,9... | collective-permute-start | bytes 1572872 | tf_op jit(solution)/shard_map/ppermute | solution.py:15
  88.3 1.2 pad_maximum_fusion.1
  89.5 70.8 %while.31 = (s32[]{:T(128)}, f32[16]{0:T(128)S(1)}, f32[8,64,512]{2,1,0:T(8,128)S(1)}, s32[16]{0:T(128)S(1)}, s32[]{:T(128)}, /*index=5*/s32[]{:T(128)}, s32[]{:T(128)}) while((s32[]{:T(128)}, f32[16]{0:T(128)S(1)}, f32[8,64,512]{2,1,0:T(8,128)S(1)}, s32[16]{0:T(128)S(1)}, s32[]{:T(128)}, /*index=5*/s32[]{:T(128)}, s32[]{:T(128)}) %tuple.58), condition=%wide.region_5.6_spmd, body=%wide.region_3.5_spmd.sunk | while | flops 262148 | bytes 1048719 | solution.py:32
  92.2 0.9 multiply_reduce_fusion.10
  96.6 0.9 multiply_reduce_fusion.10
  101.1 0.9 multiply_reduce_fusion.10
  105.5 0.9 multiply_reduce_fusion.10
  109.9 0.9 multiply_reduce_fusion.10
  114.3 0.9 multiply_reduce_fusion.10
  118.8 0.9 multiply_reduce_fusion.10
  123.2 0.9 multiply_reduce_fusion.10
  127.6 0.9 multiply_reduce_fusion.10
  132.1 0.9 multiply_reduce_fusion.10
  136.5 0.9 multiply_reduce_fusion.10
  140.9 0.9 multiply_reduce_fusion.10
  145.3 0.9 multiply_reduce_fusion.10
  149.8 0.9 multiply_reduce_fusion.10
  154.2 0.9 multiply_reduce_fusion.10
  158.6 0.9 multiply_reduce_fusion.10
  160.3 1.2 pad_maximum_fusion
  161.5 64.5 %while.30 = (s32[]{:T(128)}, f32[16]{0:T(128)S(1)}, f32[8,192,256]{2,1,0:T(8,128)S(1)}, s32[16]{0:T(128)S(1)}, s32[]{:T(128)}, /*index=5*/s32[]{:T(128)}, s32[]{:T(128)}) while((s32[]{:T(128)}, f32[16]{0:T(128)S(1)}, f32[8,192,256]{2,1,0:T(8,128)S(1)}, s32[16]{0:T(128)S(1)}, s32[]{:T(128)}, /*index=5*/s32[]{:T(128)}, s32[]{:T(128)}) %tuple.59), condition=%wide.region_2.3_spmd, body=%wide.region_0.2_spmd.sunk | while | flops 262148 | bytes 1048719 | solution.py:32
  226.0 6.5 %all-reduce.2 = (f32[3,16]{1,0:T(4,128)S(1)}, f32[3]{0:T(128)S(1)}) all-reduce(f32[3,16]{1,0:T(4,128)S(1)} %pad_maximum_fusion.2, f32[3]{0:T(128)S(1)} %pad_maximum_fusion.4), channel_id=1, replica_groups=mesh['gy_0'=4,'gy_1'=2,'gx_0'=2,'gx_1'=8,'gx_2'=2] {'gy_0'}, use_global_device_ids=true, to_apply=%region_9.10 | all-reduce | flops 51 | bytes 408 | tf_op jit(solution)/shard_map/psum | solution.py:20
  232.5 5.3 %all-reduce.5 = (f32[3,16]{1,0:T(4,128)S(1)}, f32[3]{0:T(128)S(1)}) all-reduce(f32[3,16]{1,0:T(4,128)S(1)} %get-tuple-element.107, f32[3]{0:T(128)S(1)} %get-tuple-element.108), channel_id=1, replica_groups=mesh['gy_0'=4,'gy_1'=2,'gx_0'=2,'gx_1'=8,'gx_2'=2] {'gy_1'}, use_global_device_ids=true, to_apply=%region_10.11 | all-reduce | flops 51 | bytes 408 | tf_op jit(solution)/shard_map/psum | solution.py:20
  237.7 3.8 %all-reduce.4 = (f32[3,16]{1,0:T(4,128)S(1)}, f32[3]{0:T(128)S(1)}) all-reduce(f32[3,16]{1,0:T(4,128)S(1)} %get-tuple-element.113, f32[3]{0:T(128)S(1)} %get-tuple-element.114), channel_id=1, replica_groups=mesh['gy_0'=4,'gy_1'=2,'gx_0'=2,'gx_1'=8,'gx_2'=2] {'gx_0'}, use_global_device_ids=true, to_apply=%region_11.12 | all-reduce | flops 51 | bytes 408 | tf_op jit(solution)/shard_map/psum | solution.py:20
  241.5 10.7 %all-reduce.1 = (f32[3,16]{1,0:T(4,128)S(1)}, f32[3]{0:T(128)S(1)}) all-reduce(f32[3,16]{1,0:T(4,128)S(1)} %get-tuple-element.111, f32[3]{0:T(128)S(1)} %get-tuple-element.112), channel_id=1, replica_groups=mesh['gy_0'=4,'gy_1'=2,'gx_0'=2,'gx_1'=8,'gx_2'=2] {'gx_1'}, use_global_device_ids=true, to_apply=%region_12.13 | all-reduce | flops 51 | bytes 408 | tf_op jit(solution)/shard_map/psum | solution.py:20
  252.2 10.6 %all-reduce.3 = (f32[3,16]{1,0:T(4,128)S(1)}, f32[3]{0:T(128)S(1)}) all-reduce(f32[3,16]{1,0:T(4,128)S(1)} %get-tuple-element.105, f32[3]{0:T(128)S(1)} %get-tuple-element.106), channel_id=1, replica_groups=mesh['gy_0'=4,'gy_1'=2,'gx_0'=2,'gx_1'=8,'gx_2'=2] {'gx_2'}, use_global_device_ids=true, to_apply=%region_13.14 | all-reduce | flops 51 | bytes 408 | tf_op jit(solution)/shard_map/psum | solution.py:20
  264.2 1.2 slice_divide_fusion.1
  (153 shorter events, 97.7 us)
Async XLA Ops:
  0.0 7.8 %copy-start = (f32[8,64,256]{2,1,0:T(8,128)S(1)}, f32[8,64,256]{2,1,0:T(8,128)}, u32[]{:S(2)}) copy-start(f32[8,64,256]{2,1,0:T(8,128)} %param.14) | copy-start | bytes 1572868
  0.0 7.8 %copy-start.3 = (s32[16]{0:T(128)S(1)}, s32[16]{0:T(128)}, u32[]{:S(2)}) copy-start(s32[16]{0:T(128)} %param.17) | copy-start | bytes 196
  0.0 82.0 %collective-permute-start = (f32[8,64,256]{2,1,0:T(8,128)}, f32[8,64,256]{2,1,0:T(8,128)S(1)}, u32[]{:S(2)}, u32[]{:S(2)}) collective-permute-start(f32[8,64,256]{2,1,0:T(8,128)} %param.12), channel_id=1, source_target_pairs={{0,31},{1,0},{2,1},{3,2},{4,3},{5,4},{6,5},{7,6},{8,7},{9,8},{10,9... | collective-permute-start | bytes 1572872 | tf_op jit(solution)/shard_map/ppermute | solution.py:15
  3.2 85.1 %collective-permute-start.2 = (f32[8,64,256]{2,1,0:T(8,128)}, f32[8,64,256]{2,1,0:T(8,128)}, u32[]{:S(2)}, u32[]{:S(2)}) collective-permute-start(f32[8,64,256]{2,1,0:T(8,128)} %param.13), channel_id=1, source_target_pairs={{0,224},{32,0},{64,32},{96,64},{128,96},{160,128},{192,160},{224,1... | collective-permute-start | bytes 1572872 | tf_op jit(solution)/shard_map/ppermute | solution.py:15
  7.9 69.9 %copy-start.1 = (f32[8,64,256]{2,1,0:T(8,128)S(1)}, f32[8,64,256]{2,1,0:T(8,128)}, u32[]{:S(2)}) copy-start(f32[8,64,256]{2,1,0:T(8,128)} %param.13) | copy-start | bytes 1572868
  7.9 71.4 %copy-start.2 = (f32[8,64,256]{2,1,0:T(8,128)S(1)}, f32[8,64,256]{2,1,0:T(8,128)}, u32[]{:S(2)}) copy-start(f32[8,64,256]{2,1,0:T(8,128)} %param.12) | copy-start | bytes 1572868
  78.4 11.0 %copy-start.4 = (s32[16]{0:T(128)S(1)}, s32[16]{0:T(128)}, u32[]{:S(2)}) copy-start(s32[16]{0:T(128)} %param.16) | copy-start | bytes 196
  82.0 78.3 %collective-permute-start.1 = (f32[8,64,256]{2,1,0:T(8,128)S(1)}, f32[8,64,256]{2,1,0:T(8,128)}, u32[]{:S(2)}, u32[]{:S(2)}) collective-permute-start(f32[8,64,256]{2,1,0:T(8,128)S(1)} %collective-permute-done), channel_id=1, source_target_pairs={{0,31},{1,0},{2,1},{3,2},{4,3},{5,4},{6,5},{7,6},{8,7},{9,8},{10,9... | collective-permute-start | bytes 1572872 | tf_op jit(solution)/shard_map/ppermute | solution.py:15
  160.3 1.2 copy-start.5
where the time goes:
time: 268 us; the launch traced here: 266 us
  loops' own time  97.6 us (36%)
  local copies, waits for them, and re-layouts  70.1 us (26%)
  other arithmetic  48.4 us (18%)
  blocking collectives  36.8 us (14%)
  starting transfers between devices  12.9 us (5%)
    another operation x2, loops' own time, lag_sums(): return lax.map(one_lag, (leading, lag_values))  64.4 us
    dynamic_update_slice x48, local copies, waits for them, and re-layouts, lag_sums(): return lax.map(one_lag, (leading, lag_values))  37.7 us
    psum x5, blocking collectives, by_axis(): x = lax.psum(x, axis)  36.8 us
    another operation x1, loops' own time, local(): sums_z = lax.map(along_z, sep_z)  33.3 us
    dynamic_slice x48, local copies, waits for them, and re-layouts, lag_sums(): return lax.map(one_lag, (leading, lag_values))  30.6 us
    reduce_sum x32, other arithmetic, one_lag(): return jnp.sum(head * tail)  26.2 us
    reduce_sum x16, other arithmetic, along_z(): return jnp.sum(w_field * shifted)  13.1 us
    ppermute x3, starting transfers between devices, from_behind(): return lax.ppermute(value, axis, pairs)  12.9 us
  transfers between devices with their start and end apart: 3, of which 0 were waited for; matrix products, arithmetic and copies ran while one was open for 30% of the time, Pallas kernels for 0%

commit v1 on v0

v1 whole, which is shorter than its diff:
```python
import functools

import jax
import jax.numpy as jnp
from jax import lax
from jax.experimental import pallas as pl
from jax.experimental.pallas import tpu as pltpu
from jax.sharding import PartitionSpec as P

F32 = jnp.float32
BF16 = jnp.bfloat16
MESH = pl.DeviceIdType.MESH
NT = (((1,), (1,)), ((), ()))
TN = (((0,), (0,)), ((), ()))


def place(x, y, z, core):
    return {"gy": y * 2 + x // 2, "gx": (x % 2) * 16 + z * 2 + core}


def split(value):
    high = value.astype(BF16)
    low = (value - high.astype(F32)).astype(BF16)
    return high, low


def gram(a, b, dims):
    dot = functools.partial(lax.dot_general, dimension_numbers=dims, preferred_element_type=F32)
    return dot(a[0], b[0]) + (dot(a[0], b[1]) + dot(a[1], b[0]))


def lag_row(block):
    total = block[0:8]
    for start in range(8, 128, 8):
        total += pltpu.roll(block[start:start + 8], 128 - start, 1)
    row = lax.broadcasted_iota(jnp.int32, (8, 128), 0)
    for bit in (1, 2, 4):
        total = jnp.where(row & bit != 0, pltpu.roll(total, 128 - bit, 1), total)
    return jnp.sum(total, axis=0, keepdims=True)


def kernel(u_hbm, v_hbm, w_hbm, sx_ref, sy_ref, sz_ref, out_ref,
           u_own, v_own, w_own, u_chip, u_near, v_pair, v_fwd, tile, got1, mid, got2,
           load_sem, send_sem, d2d_sem, u_sem, v_sem, y_sem, red_send, red_recv):
    gy = lax.axis_index("gy")
    gx = lax.axis_index("gx")
    y, x_hi = gy // 2, gy % 2
    x_lo, z, core = gx // 16, (gx // 2) % 8, gx % 2
    x = x_hi * 2 + x_lo
    ring = x_lo * 8 + z
    after, before = (ring + 1) % 16, (ring + 15) % 16

    def chip_u(pos, c):
        return {"gy": gy, "gx": pos * 2 + c}

    def group1(i):
        return {"gy": gy, "gx": x_lo * 16 + (gx % 16 + i) % 16}

    own2 = x * 4 + y

    def group2(i):
        other = (own2 + i) % 16
        return place(other // 4, other % 4, z, core)

    loads = [
        pltpu.make_async_copy(v_hbm, v_own, load_sem.at[0]),
        pltpu.make_async_copy(u_hbm, u_own, load_sem.at[1]),
        pltpu.make_async_copy(
            u_hbm.at[pl.ds(4 * core, 4)], u_chip.at[:, pl.ds(64 * core, 64), :], load_sem.at[2]),
        pltpu.make_async_copy(w_hbm, w_own, load_sem.at[3]),
    ]
    for load in loads:
        load.start()

    barrier = pltpu.get_barrier_semaphore()
    for pos in (after, before):
        for c in range(2):
            pl.semaphore_signal(barrier, inc=1, device_id=chip_u(pos, c), device_id_type=MESH)

    def greet(i, carry):
        pl.semaphore_signal(barrier, inc=1, device_id=group1(i), device_id_type=MESH)
        pl.semaphore_signal(barrier, inc=1, device_id=group2(i), device_id_type=MESH)
        return carry

    lax.fori_loop(1, 16, greet, 0)
    pl.semaphore_wait(barrier, 34)

    sends = []

    def send(src, dst, sem, target):
        copy = pltpu.make_async_remote_copy(
            src_ref=src, dst_ref=dst, send_sem=send_sem.at[len(sends)], recv_sem=sem,
            device_id=target, device_id_type=MESH)
        copy.start()
        sends.append(copy)

    loads[0].wait()
    for chunk in range(2):
        lead = (x_hi + chunk) % 2 * 2
        for step in (1, 3):
            other = (x + step) % 4
            base = ((other + 3) % 4) // 2 * 4
            send(v_own.at[pl.ds(base + lead, 2)], v_pair.at[x_hi, pl.ds(lead, 2)],
                 v_sem.at[x_hi, chunk], place(other, y, z, core))
    loads[1].wait()
    rows = pl.ds(64 * core, 64)
    for c in range(2):
        send(u_own.at[pl.ds(4 * c, 2)], u_near.at[pl.ds(0, 2), rows, :], u_sem.at[0, core], chip_u(before, c))
        send(u_own.at[pl.ds(4 * c + 2, 2)], u_near.at[pl.ds(2, 2), rows, :], u_sem.at[1, core], chip_u(after, c))
    send(u_own.at[pl.ds(4 * (1 - core), 4)], u_chip.at[:, rows, :], d2d_sem, chip_u(ring, 1 - core))

    def landed(ref, sem):
        pltpu.make_async_copy(ref, ref, sem).wait()

    loads[3].wait()
    energy_u = jnp.zeros((64, 256), F32)
    energy_v = jnp.zeros((64, 256), F32)
    for p in range(8):
        energy_u += u_own[p] * u_own[p]
        energy_v += v_own[p] * v_own[p]
    z_sums = []
    for lag in range(5):
        total = jnp.zeros((64, 256), F32)
        for p in range(8 - lag):
            total += w_own[p] * w_own[p + lag]
        z_sums.append(total)
    lane = lax.broadcasted_iota(jnp.int32, (1, 128), 1)
    scalars = jnp.zeros((1, 128), F32)
    for i, total in enumerate([energy_u, energy_v] + z_sums):
        scalars = jnp.where(lane == i, jnp.sum(total), scalars)

    v_split = split(v_own[...].reshape(512, 256))
    v_same = gram(v_split, v_split, TN)

    loads[2].wait()
    landed(u_chip.at[:, rows, :], d2d_sem)
    u_same = jnp.zeros((128, 128), F32)
    u_parts = [split(u_chip[p]) for p in range(4)]
    for p in range(4):
        u_same += gram(u_parts[p], u_parts[p], NT)

    landed(v_pair.at[0, pl.ds(0, 2)], v_sem.at[0, 0])
    send(v_pair.at[0, pl.ds(0, 2)], v_fwd.at[pl.ds(0, 2)], y_sem.at[0], place(x, (y + 3) % 4, z, core))
    landed(v_pair.at[1, pl.ds(2, 2)], v_sem.at[1, 0])
    send(v_pair.at[1, pl.ds(2, 2)], v_fwd.at[pl.ds(2, 2)], y_sem.at[1], place(x, (y + 1) % 4, z, core))

    landed(v_pair.at[0, pl.ds(2, 2)], v_sem.at[0, 1])
    landed(v_pair.at[1, pl.ds(0, 2)], v_sem.at[1, 1])
    left = split(v_pair[0].reshape(256, 256))
    right = split(v_pair[1].reshape(256, 256))
    v_cross = gram(left, right, TN)

    u_cross = jnp.zeros((128, 128), F32)
    for c in range(2):
        landed(u_near.at[pl.ds(0, 2), pl.ds(64 * c, 64), :], u_sem.at[0, c])
        landed(u_near.at[pl.ds(2, 2), pl.ds(64 * c, 64), :], u_sem.at[1, c])
    for p in range(4):
        part = split(u_near[p])
        mine = split(u_chip[p])
        u_cross += gram(mine, part, NT) if p < 2 else gram(part, mine, NT)

    landed(v_fwd.at[pl.ds(0, 2)], y_sem.at[0])
    landed(v_fwd.at[pl.ds(2, 2)], y_sem.at[1])
    first = split(v_fwd[0:2].reshape(128, 256))
    second = split(v_fwd[2:4].reshape(128, 256))
    here_right = split(v_pair[1, 0:2].reshape(128, 256))
    here_left = split(v_pair[0, 2:4].reshape(128, 256))
    v_cross += gram(here_right, first, TN)
    v_cross += gram(second, here_left, TN)

    row = lax.broadcasted_iota(jnp.int32, (128, 128), 0)
    col = lax.broadcasted_iota(jnp.int32, (128, 128), 1)
    u_block = jnp.where(col > row, u_same, u_cross)
    near = jnp.where(col > row, v_same[:128, :128] + v_same[128:, 128:], v_cross[:128, :128] + v_cross[128:, 128:])
    far = v_same[:128, 128:] + v_cross[128:, :128]
    tile[0:1] = lag_row(u_block)
    tile[1:2] = lag_row(jnp.where(col < row, far, near))
    tile[2:3] = lag_row(jnp.where(col < row, near, far))
    tile[3:4] = scalars

    def all_sum(src, got, own, group, index):
        got[own] = src[...]

        def one(i, carry):
            pltpu.make_async_remote_copy(
                src_ref=src, dst_ref=got.at[own], send_sem=red_send.at[index], recv_sem=red_recv.at[index],
                device_id=group(i), device_id_type=MESH).start()
            return carry

        lax.fori_loop(1, 16, one, 0)
        landed(got.at[pl.ds(0, 15)], red_recv.at[index])
        return jnp.sum(got[...], axis=0)

    mid[...] = all_sum(tile, got1, gx % 16, group1, 0)
    sums = all_sum(mid, got2, own2, group2, 1)

    sums = jnp.concatenate([sums, jnp.zeros((4, 128), F32)], axis=0)
    lag = lax.broadcasted_iota(jnp.int32, (128, 16), 0)

    def pick(sep):
        chosen = jnp.where(lag == sep, 1.0, 0.0).astype(F32)
        return lax.dot_general(sums, chosen, (((1,), (0,)), ((), ())),
                               precision=lax.Precision.HIGHEST, preferred_element_type=F32)

    sep_x, sep_y, sep_z = sx_ref[...], sy_ref[...], sz_ref[...]
    along_x = pick(sep_x % 128)[0:1]
    both_y = pick(sep_y % 128)
    along_y = jnp.where((sep_y >= 128) & (sep_y < 256), both_y[2:3], both_y[1:2])
    along_z = pick(sep_z + 2)[3:4]
    planes = 8.0
    out_ref[0:1] = along_x / sums[3:4, 0:1]
    out_ref[1:2] = along_y / sums[3:4, 1:2]
    out_ref[2:3] = along_z / sums[3:4, 2:3] * (planes / (planes - sep_z.astype(F32)))

    for copy in sends:
        copy.wait_send()
    landed(got1.at[pl.ds(0, 15)], red_send.at[0])
    landed(got2.at[pl.ds(0, 15)], red_send.at[1])


def local(u_field, v_field, w_field, sep_x, sep_y, sep_z):
    vmem = pl.BlockSpec(memory_space=pltpu.VMEM)
    hbm = pl.BlockSpec(memory_space=pl.ANY)
    block = (8, 64, 256)
    return pl.pallas_call(
        kernel,
        out_shape=jax.ShapeDtypeStruct((3, 16), F32),
        in_specs=[hbm] * 3 + [vmem] * 3,
        out_specs=vmem,
        scratch_shapes=[
            pltpu.VMEM(block, F32),
            pltpu.VMEM(block, F32),
            pltpu.VMEM(block, F32),
            pltpu.VMEM((4, 128, 256), F32),
            pltpu.VMEM((4, 128, 256), F32),
            pltpu.VMEM((2, 4, 64, 256), F32),
            pltpu.VMEM((4, 64, 256), F32),
            pltpu.VMEM((4, 128), F32),
            pltpu.VMEM((16, 4, 128), F32),
            pltpu.VMEM((4, 128), F32),
            pltpu.VMEM((16, 4, 128), F32),
            pltpu.SemaphoreType.DMA((4,)),
            pltpu.SemaphoreType.DMA((12,)),
            pltpu.SemaphoreType.DMA,
            pltpu.SemaphoreType.DMA((2, 2)),
            pltpu.SemaphoreType.DMA((2, 2)),
            pltpu.SemaphoreType.DMA((2,)),
            pltpu.SemaphoreType.DMA((2,)),
            pltpu.SemaphoreType.DMA((2,)),
        ],
        compiler_params=pltpu.CompilerParams(collective_id=0, has_side_effects=True),
    )(u_field, v_field, w_field, sep_x.reshape(1, 16), sep_y.reshape(1, 16), sep_z.reshape(1, 16))


def solution(mesh):
    placed = (P(None, "gx", "gy"),) * 3 + (P(),) * 3
    return jax.shard_map(local, mesh=mesh, in_specs=placed, out_specs=P(), check_vma=False)
```

time: 268 us -> 37 us (0.14)
  loops' own time: 97.6 us -> 0 us
  local copies, waits for them, and re-layouts: 70.1 us -> 1.26 us
  other arithmetic: 48.4 us -> 0 us
  blocking collectives: 36.8 us -> 0 us
  Pallas kernels: 0 us -> 35.6 us
  starting transfers between devices: 12.9 us -> 0 us
    another operation x3 -> x0, loops' own time: 97.6 us -> none  [the longest x2 64.4 us: lag_sums(): return lax.map(one_lag, (leading, lag_values))]
    reduce_sum x51 -> x0, other arithmetic: 41.6 us -> none  [the longest x32 26.2 us: one_lag(): return jnp.sum(head * tail)]
    dynamic_update_slice x48 -> x0, local copies, waits for them, and re-layouts: 37.7 us -> none  [lag_sums(): return lax.map(one_lag, (leading, lag_values))]
    psum x5 -> x0, blocking collectives: 36.8 us -> none  [by_axis(): x = lax.psum(x, axis)]
    pallas_call x0 -> x1, Pallas kernels: none -> 35.6 us  [local(): pl.pallas_call(kernel, out_shape=jax.ShapeDtypeStruct((3, 16), F32), in_s...]
    dynamic_slice x48 -> x0, local copies, waits for them, and re-layouts: 30.6 us -> none  [lag_sums(): return lax.map(one_lag, (leading, lag_values))]
    ppermute x3 -> x0, starting transfers between devices: 12.9 us -> none  [from_behind(): return lax.ppermute(value, axis, pairs)]
    another operation x4 -> x0, other arithmetic: 3.26 us -> none  [the longest x1 1.96 us: local(): jnp.stack([jnp.sum(u_field * u_field), jnp.sum(v_field * v_field), jnp.su...]
  transfers between devices with their start and end apart: 3 -> 0, of which waited for: 0 -> 0; matrix products, arithmetic and copies ran while one was open for 30% -> 0% of each run, Pallas kernels for 0% -> 0%
where the time goes in v1:
time: 37 us; the launch traced here: 36.9 us
  Pallas kernels  35.6 us (96%)
  local copies, waits for them, and re-layouts  1.26 us (3%)
    pallas_call x1, Pallas kernels, local(): pl.pallas_call(kernel, out_shape=jax.ShapeDtypeStruct((3, 16), F32), in_s...  35.6 us
    unnamed x1, local copies, waits for them, and re-layouts  1.26 us

profile of v1, /device:TPU:1, one launch (start us, length us, event | category | flops | bytes accessed | tf_op | source)
XLA Modules:
  0.0 36.9 jit_solution(7297756387839330225)
XLA Ops:
  0.0 35.6 %shard_map.64 = f32[3,16]{1,0:T(4,128)} custom-call(f32[8,64,256]{2,1,0:T(8,128)} %u_hbm.1, f32[8,64,256]{2,1,0:T(8,128)} %v_hbm.1, f32[8,64,256]{2,1,0:T(8,128)} %w_hbm.1, s32[1,16]{1,0:T(1,128)} %bitcast.3, s32[1,16]{1,0:T(1,128)} %bitcast.4, s32[1,16]{1,0:T(1,128)} %bitcast.5), custom_call_target="tpu_custom_call" | custom-call | tf_op jit(solution)/shard_map/pallas_call | solution.py:225
  35.6 1.3 %copy.8 = f32[3,16]{1,0:T(4,128)} copy(f32[3,16]{1,0:T(4,128)} %shard_map.64) | data formatting | bytes 384

commit v2 on v1

--- a/solution.py
+++ b/solution.py
@@ -40,8 +40,8 @@
 
 
 def kernel(u_hbm, v_hbm, w_hbm, sx_ref, sy_ref, sz_ref, out_ref,
-           u_own, v_own, w_own, u_chip, u_near, v_pair, v_fwd, tile, got1, mid, got2,
-           load_sem, send_sem, d2d_sem, u_sem, v_sem, y_sem, red_send, red_recv):
+           u_own, v_own, w_own, u_chip, u_near, u_extra, u_sum, v_pair, v_fwd, tile, got1, mid, got2,
+           load_sem, send_sem, d2d_sem, u_sem, extra_sem, v_sem, y_sem, red_send, red_recv, token):
     gy = lax.axis_index("gy")
     gx = lax.axis_index("gx")
     y, x_hi = gy // 2, gy % 2
@@ -72,45 +72,77 @@
     for load in loads:
         load.start()
 
+    beside = [place((x + 1) % 4, y, z, core), place((x + 3) % 4, y, z, core),
+              place(x, (y + 1) % 4, z, core), place(x, (y + 3) % 4, z, core),
+              place(x, y, (z + 1) % 8, core), place(x, y, (z + 7) % 8, core)]
+    others = [place(x, y, z, 1 - core), place(x, y, (z + 1) % 8, 1 - core), place(x, y, (z + 7) % 8, 1 - core)]
+    others += [chip_u(pos, c) for pos in (after, before) for c in range(2)]
     barrier = pltpu.get_barrier_semaphore()
-    for pos in (after, before):
-        for c in range(2):
-            pl.semaphore_signal(barrier, inc=1, device_id=chip_u(pos, c), device_id_type=MESH)
-
-    def greet(i, carry):
-        pl.semaphore_signal(barrier, inc=1, device_id=group1(i), device_id_type=MESH)
-        pl.semaphore_signal(barrier, inc=1, device_id=group2(i), device_id_type=MESH)
-        return carry
-
-    lax.fori_loop(1, 16, greet, 0)
-    pl.semaphore_wait(barrier, 34)
+    for target in beside + others:
+        pl.semaphore_signal(barrier, inc=1, device_id=target, device_id_type=MESH)
+    pl.semaphore_wait(barrier, len(beside) + len(others))
+
+    def tell(step):
+        for target in beside:
+            pl.semaphore_signal(token.at[step], inc=1, device_id=target, device_id_type=MESH)
+
+    def told(step):
+        pl.semaphore_wait(token.at[step], len(beside))
 
     sends = []
 
-    def send(src, dst, sem, target):
-        copy = pltpu.make_async_remote_copy(
-            src_ref=src, dst_ref=dst, send_sem=send_sem.at[len(sends)], recv_sem=sem,
+    def remote(src, dst, sem, target, slot):
+        return pltpu.make_async_remote_copy(
+            src_ref=src, dst_ref=dst, send_sem=send_sem.at[slot], recv_sem=sem,
             device_id=target, device_id_type=MESH)
+
+    def send(*args):
+        copy = remote(*args, len(sends))
         copy.start()
         sends.append(copy)
 
+    def landed(ref, sem):
+        pltpu.make_async_copy(ref, ref, sem).wait()
+
+    first_last, last_first = z == 0, z == 7
+    rows = pl.ds(64 * core, 64)
+
+    def to_before(c, k):
+        return (u_own.at[4 * c + k], u_near.at[k, rows, :], u_sem.at[0, k, core], chip_u(before, c))
+
+    def to_after(c, k):
+        return (u_own.at[4 * c + 3 - k], u_near.at[3 - k, rows, :], u_sem.at[1, k, core], chip_u(after, c))
+
+    def to_close(c):
+        return (u_own.at[4 * c + 2], u_extra.at[rows, :], extra_sem.at[core], chip_u(before, c))
+
     loads[0].wait()
-    for chunk in range(2):
-        lead = (x_hi + chunk) % 2 * 2
+    loads[1].wait()
+    for j in range(4):
+        lead = (x_hi * 2 + j) % 4
         for step in (1, 3):
             other = (x + step) % 4
             base = ((other + 3) % 4) // 2 * 4
-            send(v_own.at[pl.ds(base + lead, 2)], v_pair.at[x_hi, pl.ds(lead, 2)],
-                 v_sem.at[x_hi, chunk], place(other, y, z, core))
-    loads[1].wait()
-    rows = pl.ds(64 * core, 64)
+            send(v_own.at[base + lead], v_pair.at[x_hi, lead], v_sem.at[x_hi, j], place(other, y, z, core))
+        if j == 0:
+            send(u_own.at[pl.ds(4 * (1 - core), 4)], u_chip.at[:, rows, :], d2d_sem, chip_u(ring, 1 - core))
+        if j == 1 or j == 3:
+            k = j // 2
+            for c in range(2):
+                send(*to_before(c, k))
+                if k == 0:
+                    send(*to_after(c, k))
+    base_slot = len(sends) + 4
     for c in range(2):
-        send(u_own.at[pl.ds(4 * c, 2)], u_near.at[pl.ds(0, 2), rows, :], u_sem.at[0, core], chip_u(before, c))
-        send(u_own.at[pl.ds(4 * c + 2, 2)], u_near.at[pl.ds(2, 2), rows, :], u_sem.at[1, core], chip_u(after, c))
-    send(u_own.at[pl.ds(4 * (1 - core), 4)], u_chip.at[:, rows, :], d2d_sem, chip_u(ring, 1 - core))
-
-    def landed(ref, sem):
-        pltpu.make_async_copy(ref, ref, sem).wait()
+        @pl.when(jnp.logical_not(last_first))
+        def _():
+            remote(*to_after(c, 1), base_slot + c).start()
+
+        @pl.when(first_last)
+        def _():
+            remote(*to_close(c), base_slot + 2 + c).start()
+
+    tell(0)
 
     loads[3].wait()
     energy_u = jnp.zeros((64, 256), F32)
@@ -128,55 +160,77 @@
     scalars = jnp.zeros((1, 128), F32)
     for i, total in enumerate([energy_u, energy_v] + z_sums):
         scalars = jnp.where(lane == i, jnp.sum(total), scalars)
-
+    tile[3:4] = scalars
+
+    told(0)
+    tell(1)
     v_split = split(v_own[...].reshape(512, 256))
     v_same = gram(v_split, v_split, TN)
 
     loads[2].wait()
     landed(u_chip.at[:, rows, :], d2d_sem)
     u_same = jnp.zeros((128, 128), F32)
-    u_parts = [split(u_chip[p]) for p in range(4)]
     for p in range(4):
-        u_same += gram(u_parts[p], u_parts[p], NT)
-
-    landed(v_pair.at[0, pl.ds(0, 2)], v_sem.at[0, 0])
-    send(v_pair.at[0, pl.ds(0, 2)], v_fwd.at[pl.ds(0, 2)], y_sem.at[0], place(x, (y + 3) % 4, z, core))
-    landed(v_pair.at[1, pl.ds(2, 2)], v_sem.at[1, 0])
-    send(v_pair.at[1, pl.ds(2, 2)], v_fwd.at[pl.ds(2, 2)], y_sem.at[1], place(x, (y + 1) % 4, z, core))
-
-    landed(v_pair.at[0, pl.ds(2, 2)], v_sem.at[0, 1])
-    landed(v_pair.at[1, pl.ds(0, 2)], v_sem.at[1, 1])
-    left = split(v_pair[0].reshape(256, 256))
-    right = split(v_pair[1].reshape(256, 256))
-    v_cross = gram(left, right, TN)
-
-    u_cross = jnp.zeros((128, 128), F32)
-    for c in range(2):
-        landed(u_near.at[pl.ds(0, 2), pl.ds(64 * c, 64), :], u_sem.at[0, c])
-        landed(u_near.at[pl.ds(2, 2), pl.ds(64 * c, 64), :], u_sem.at[1, c])
-    for p in range(4):
-        part = split(u_near[p])
-        mine = split(u_chip[p])
-        u_cross += gram(mine, part, NT) if p < 2 else gram(part, mine, NT)
-
-    landed(v_fwd.at[pl.ds(0, 2)], y_sem.at[0])
-    landed(v_fwd.at[pl.ds(2, 2)], y_sem.at[1])
-    first = split(v_fwd[0:2].reshape(128, 256))
-    second = split(v_fwd[2:4].reshape(128, 256))
-    here_right = split(v_pair[1, 0:2].reshape(128, 256))
-    here_left = split(v_pair[0, 2:4].reshape(128, 256))
-    v_cross += gram(here_right, first, TN)
-    v_cross += gram(second, here_left, TN)
+        part = split(u_chip[p])
+        u_same += gram(part, part, NT)
+    told(1)
+    tell(2)
+
+    for k in range(2):
+        landed(v_pair.at[0, k], v_sem.at[0, k])
+        send(v_pair.at[0, k], v_fwd.at[k], y_sem.at[0, k], place(x, (y + 3) % 4, z, core))
+        landed(v_pair.at[1, 2 + k], v_sem.at[1, k])
+        send(v_pair.at[1, 2 + k], v_fwd.at[2 + k], y_sem.at[1, k], place(x, (y + 1) % 4, z, core))
+
+    def near_u(k):
+        for c in range(2):
+            half = pl.ds(64 * c, 64)
+            landed(u_near.at[k, half, :], u_sem.at[0, k, c])
+
+            def other_side():
+                landed(u_near.at[3 - k, half, :], u_sem.at[1, k, c])
+
+            if k == 0:
+                other_side()
+            else:
+                pl.when(jnp.logical_not(first_last))(other_side)
+
+                @pl.when(last_first)
+                def _():
+                    landed(u_extra.at[half, :], extra_sem.at[c])
+
+    def cross_v(k):
+        landed(v_pair.at[1, k], v_sem.at[1, 2 + k])
+        landed(v_pair.at[0, 2 + k], v_sem.at[0, 2 + k])
+        landed(v_fwd.at[k], y_sem.at[0, k])
+        landed(v_fwd.at[2 + k], y_sem.at[1, k])
+        a = [v_pair[0, k], v_pair[0, 2 + k], v_pair[1, k], v_fwd[2 + k]]
+        b = [v_pair[1, k], v_pair[1, 2 + k], v_fwd[k], v_pair[0, 2 + k]]
+        return gram(split(jnp.concatenate(a, axis=0)), split(jnp.concatenate(b, axis=0)), TN)
+
+    near_u(0)
+    u_sum[...] = gram(split(u_chip[0]), split(u_near[0]), NT) + gram(split(u_near[3]), split(u_chip[3]), NT)
+    v_cross = cross_v(0)
+    near_u(1)
+    u_sum[...] += gram(split(u_chip[1]), split(u_near[1]), NT)
+
+    @pl.when(jnp.logical_not(first_last))
+    def _():
+        u_sum[...] += gram(split(u_near[2]), split(u_chip[2]), NT)
+
+    @pl.when(last_first)
+    def _():
+        u_sum[...] += gram(split(u_chip[2]), split(u_extra[...]), NT)
 
     row = lax.broadcasted_iota(jnp.int32, (128, 128), 0)
     col = lax.broadcasted_iota(jnp.int32, (128, 128), 1)
-    u_block = jnp.where(col > row, u_same, u_cross)
+    tile[0:1] = lag_row(jnp.where(col > row, u_same, u_sum[...]))
+    v_cross += cross_v(1)
     near = jnp.where(col > row, v_same[:128, :128] + v_same[128:, 128:], v_cross[:128, :128] + v_cross[128:, 128:])
     far = v_same[:128, 128:] + v_cross[128:, :128]
-    tile[0:1] = lag_row(u_block)
     tile[1:2] = lag_row(jnp.where(col < row, far, near))
     tile[2:3] = lag_row(jnp.where(col < row, near, far))
-    tile[3:4] = scalars
+    told(2)
 
     def all_sum(src, got, own, group, index):
         got[own] = src[...]
@@ -214,6 +268,15 @@
 
     for copy in sends:
         copy.wait_send()
+    for c in range(2):
+        @pl.when(jnp.logical_not(last_first))
+        def _():
+            remote(*to_after(c, 1), base_slot + c).wait_send()
+
+        @pl.when(first_last)
+        def _():
+            remote(*to_close(c), base_slot + 2 + c).wait_send()
+
     landed(got1.at[pl.ds(0, 15)], red_send.at[0])
     landed(got2.at[pl.ds(0, 15)], red_send.at[1])
 
@@ -233,6 +296,8 @@
             pltpu.VMEM(block, F32),
             pltpu.VMEM((4, 128, 256), F32),
             pltpu.VMEM((4, 128, 256), F32),
+            pltpu.VMEM((128, 256), F32),
+            pltpu.VMEM((128, 128), F32),
             pltpu.VMEM((2, 4, 64, 256), F32),
             pltpu.VMEM((4, 64, 256), F32),
             pltpu.VMEM((4, 128), F32),
@@ -240,13 +305,15 @@
             pltpu.VMEM((4, 128), F32),
             pltpu.VMEM((16, 4, 128), F32),
             pltpu.SemaphoreType.DMA((4,)),
-            pltpu.SemaphoreType.DMA((12,)),
+            pltpu.SemaphoreType.DMA((23,)),
             pltpu.SemaphoreType.DMA,
-            pltpu.SemaphoreType.DMA((2, 2)),
+            pltpu.SemaphoreType.DMA((2, 2, 2)),
+            pltpu.SemaphoreType.DMA((2,)),
+            pltpu.SemaphoreType.DMA((2, 4)),
             pltpu.SemaphoreType.DMA((2, 2)),
             pltpu.SemaphoreType.DMA((2,)),
             pltpu.SemaphoreType.DMA((2,)),
-            pltpu.SemaphoreType.DMA((2,)),
+            pltpu.SemaphoreType.REGULAR((3,)),
         ],
         compiler_params=pltpu.CompilerParams(collective_id=0, has_side_effects=True),
     )(u_field, v_field, w_field, sep_x.reshape(1, 16), sep_y.reshape(1, 16), sep_z.reshape(1, 16))

time: 37 us -> 37.8 us (1.022)
  Pallas kernels: 35.6 us -> 36.4 us
    pallas_call x1, Pallas kernels: 35.6 us -> 36.4 us  [local(): pl.pallas_call(kernel, out_shape=jax.ShapeDtypeStruct((3, 16), F32), in_s...]
where the time goes in v2:
time: 37.8 us; the launch traced here: 37.7 us
  Pallas kernels  36.4 us (96%)
  local copies, waits for them, and re-layouts  1.26 us (3%)
    pallas_call x1, Pallas kernels, local(): pl.pallas_call(kernel, out_shape=jax.ShapeDtypeStruct((3, 16), F32), in_s...  36.4 us
    unnamed x1, local copies, waits for them, and re-layouts  1.26 us

profile of v2, /device:TPU:1, one launch (start us, length us, event | category | flops | bytes accessed | tf_op | source)
XLA Modules:
  0.0 37.7 jit_solution(8014688161147103679)
XLA Ops:
  0.0 36.4 %shard_map.64 = f32[3,16]{1,0:T(4,128)} custom-call(f32[8,64,256]{2,1,0:T(8,128)} %u_hbm.1, f32[8,64,256]{2,1,0:T(8,128)} %v_hbm.1, f32[8,64,256]{2,1,0:T(8,128)} %w_hbm.1, s32[1,16]{1,0:T(1,128)} %bitcast.3, s32[1,16]{1,0:T(1,128)} %bitcast.4, s32[1,16]{1,0:T(1,128)} %bitcast.5), custom_call_target="tpu_custom_call" | custom-call | tf_op jit(solution)/shard_map/pallas_call | solution.py:288
  36.4 1.3 %copy.8 = f32[3,16]{1,0:T(4,128)} copy(f32[3,16]{1,0:T(4,128)} %shard_map.64) | data formatting | bytes 384

commit v3 on v2

--- a/solution.py
+++ b/solution.py
@@ -39,9 +39,9 @@
     return jnp.sum(total, axis=0, keepdims=True)
 
 
-def kernel(u_hbm, v_hbm, w_hbm, sx_ref, sy_ref, sz_ref, out_ref,
-           u_own, v_own, w_own, u_chip, u_near, u_extra, u_sum, v_pair, v_fwd, tile, got1, mid, got2,
-           load_sem, send_sem, d2d_sem, u_sem, extra_sem, v_sem, y_sem, red_send, red_recv, token):
+def kernel(u_hbm, v_hbm, w_hbm, sx_hbm, sy_hbm, sz_hbm, out_ref,
+           u_own, v_own, w_own, u_chip, u_near, u_extra, u_hand, u_sum, v_pair, v_fwd, tile, got1, mid, got2,
+           load_sem, send_sem, d2d_sem, u_sem, extra_sem, hand_sem, v_sem, y_sem, red_send, red_recv, token, back, sx_ref, sy_ref, sz_ref, sep_sem):
     gy = lax.axis_index("gy")
     gx = lax.axis_index("gx")
     y, x_hi = gy // 2, gy % 2
@@ -71,20 +71,45 @@
     ]
     for load in loads:
         load.start()
-
-    beside = [place((x + 1) % 4, y, z, core), place((x + 3) % 4, y, z, core),
-              place(x, (y + 1) % 4, z, core), place(x, (y + 3) % 4, z, core),
-              place(x, y, (z + 1) % 8, core), place(x, y, (z + 7) % 8, core)]
-    others = [place(x, y, z, 1 - core), place(x, y, (z + 1) % 8, 1 - core), place(x, y, (z + 7) % 8, 1 - core)]
-    others += [chip_u(pos, c) for pos in (after, before) for c in range(2)]
+    lags = [pltpu.make_async_copy(src, dst, sep_sem.at[i])
+            for i, (src, dst) in enumerate([(sx_hbm, sx_ref), (sy_hbm, sy_ref), (sz_hbm, sz_ref)])]
+    for load in lags:
+        load.start()
+
+    first, second, last = z == 0, z == 1, z == 7
+    in_plane = [place((x + 1) % 4, y, z, core), place((x + 3) % 4, y, z, core),
+                place(x, (y + 1) % 4, z, core), place(x, (y + 3) % 4, z, core), chip_u(ring, 1 - core)]
+    beside = in_plane[:4] + [place(x, y, (z + 1) % 8, core), place(x, y, (z + 7) % 8, core)]
+    wrapped = [chip_u(x_lo * 8 + 7 - z, c) for c in range(2)]
+    two_back = [chip_u((ring + 14) % 16, c) for c in range(2)]
+    two_on = [chip_u((ring + 2) % 16, c) for c in range(2)]
+    chip_before = [chip_u(before, c) for c in range(2)]
+    chip_after = [chip_u(after, c) for c in range(2)]
+    across = chip_u((ring + 8) % 16, core)
+
+    def signal(sem, targets):
+        for target in targets:
+            pl.semaphore_signal(sem, inc=1, device_id=target, device_id_type=MESH)
+
     barrier = pltpu.get_barrier_semaphore()
-    for target in beside + others:
-        pl.semaphore_signal(barrier, inc=1, device_id=target, device_id_type=MESH)
-    pl.semaphore_wait(barrier, len(beside) + len(others))
+    signal(barrier, in_plane)
+
+    @pl.when(jnp.logical_not(last))
+    def _():
+        signal(barrier, chip_after)
+
+    @pl.when(first)
+    def _():
+        signal(barrier, wrapped)
+
+    @pl.when(second)
+    def _():
+        signal(barrier, two_back)
+
+    pl.semaphore_wait(barrier, 5 + 2 * jnp.minimum(z, 1) + 4 * (z // 7))
 
     def tell(step):
-        for target in beside:
-            pl.semaphore_signal(token.at[step], inc=1, device_id=target, device_id_type=MESH)
+        signal(token.at[step], beside)
 
     def told(step):
         pl.semaphore_wait(token.at[step], len(beside))
@@ -104,45 +129,51 @@
     def landed(ref, sem):
         pltpu.make_async_copy(ref, ref, sem).wait()
 
-    first_last, last_first = z == 0, z == 7
     rows = pl.ds(64 * core, 64)
-
-    def to_before(c, k):
-        return (u_own.at[4 * c + k], u_near.at[k, rows, :], u_sem.at[0, k, core], chip_u(before, c))
-
-    def to_after(c, k):
-        return (u_own.at[4 * c + 3 - k], u_near.at[3 - k, rows, :], u_sem.at[1, k, core], chip_u(after, c))
-
-    def to_close(c):
-        return (u_own.at[4 * c + 2], u_extra.at[rows, :], extra_sem.at[core], chip_u(before, c))
+    pieces = [(k, c) for k in range(2) for c in range(2)]
+
+    def to_before(k, c):
+        return (u_own.at[4 * c + k], u_near.at[k, rows, :], u_sem.at[0, k, core], chip_before[c], 13 + 2 * k + c)
+
+    def to_after(k, c):
+        return (u_own.at[4 * c + 3 - k], u_near.at[3 - k, rows, :], u_sem.at[1, k, core], chip_after[c], 17 + 2 * k + c)
+
+    def to_across(k, c):
+        return (u_own.at[4 * c + k], u_hand.at[k, c], hand_sem.at[k, c], across, 13 + 2 * k + c)
+
+    def hand_on(k, c):
+        return (u_hand.at[k, c], u_near.at[k, rows, :], u_sem.at[0, k, core], wrapped[c], 21 + 2 * k + c)
+
+    def to_second(k, c):
+        return (u_own.at[4 * c + 3 - k], u_extra.at[1 - k, rows, :], extra_sem.at[k, core], two_on[c], 17 + 2 * k + c)
+
+    loads[1].wait()
+
+    @pl.when(first)
+    def _():
+        for piece in pieces:
+            remote(*to_across(*piece)).start()
+
+    @pl.when(jnp.logical_not(first))
+    def _():
+        for piece in pieces:
+            remote(*to_before(*piece)).start()
+        signal(back, chip_before)
+
+    @pl.when(last)
+    def _():
+        for piece in pieces:
+            remote(*to_second(*piece)).start()
+        signal(back, wrapped)
 
     loads[0].wait()
-    loads[1].wait()
     for j in range(4):
         lead = (x_hi * 2 + j) % 4
         for step in (1, 3):
             other = (x + step) % 4
             base = ((other + 3) % 4) // 2 * 4
             send(v_own.at[base + lead], v_pair.at[x_hi, lead], v_sem.at[x_hi, j], place(other, y, z, core))
-        if j == 0:
-            send(u_own.at[pl.ds(4 * (1 - core), 4)], u_chip.at[:, rows, :], d2d_sem, chip_u(ring, 1 - core))
-        if j == 1 or j == 3:
-            k = j // 2
-            for c in range(2):
-                send(*to_before(c, k))
-                if k == 0:
-                    send(*to_after(c, k))
-    base_slot = len(sends) + 4
-    for c in range(2):
-        @pl.when(jnp.logical_not(last_first))
-        def _():
-            remote(*to_after(c, 1), base_slot + c).start()
-
-        @pl.when(first_last)
-        def _():
-            remote(*to_close(c), base_slot + 2 + c).start()
-
-    tell(0)
+    send(u_own.at[pl.ds(4 * (1 - core), 4)], u_chip.at[:, rows, :], d2d_sem, chip_u(ring, 1 - core))
 
     loads[3].wait()
     energy_u = jnp.zeros((64, 256), F32)
@@ -162,8 +193,20 @@
         scalars = jnp.where(lane == i, jnp.sum(total), scalars)
     tile[3:4] = scalars
 
-    told(0)
-    tell(1)
+    @pl.when(jnp.logical_not(last))
+    def _():
+        pl.semaphore_wait(back, 2 + 2 * (1 - jnp.minimum(z, 1)))
+        for piece in pieces:
+            remote(*to_after(*piece)).start()
+
+    @pl.when(first)
+    def _():
+        for k, c in pieces:
+            landed(u_hand.at[k, c], hand_sem.at[k, c])
+            remote(*hand_on(k, c)).start()
+
+    tell(0)
+
     v_split = split(v_own[...].reshape(512, 256))
     v_same = gram(v_split, v_split, TN)
 
@@ -173,10 +216,8 @@
     for p in range(4):
         part = split(u_chip[p])
         u_same += gram(part, part, NT)
-    told(1)
-    tell(2)
-
-    for k in range(2):
+
+    def pass_on(k):
         landed(v_pair.at[0, k], v_sem.at[0, k])
         send(v_pair.at[0, k], v_fwd.at[k], y_sem.at[0, k], place(x, (y + 3) % 4, z, core))
         landed(v_pair.at[1, 2 + k], v_sem.at[1, k])
@@ -184,20 +225,18 @@
 
     def near_u(k):
         for c in range(2):
-            half = pl.ds(64 * c, 64)
-            landed(u_near.at[k, half, :], u_sem.at[0, k, c])
-
-            def other_side():
-                landed(u_near.at[3 - k, half, :], u_sem.at[1, k, c])
-
-            if k == 0:
-                other_side()
-            else:
-                pl.when(jnp.logical_not(first_last))(other_side)
-
-                @pl.when(last_first)
-                def _():
-                    landed(u_extra.at[half, :], extra_sem.at[c])
+            landed(u_near.at[k, pl.ds(64 * c, 64), :], u_sem.at[0, k, c])
+        term = gram(split(u_chip[k]), split(u_near[k]), NT)
+        if k == 0:
+            u_sum[...] = term
+        else:
+            u_sum[...] += term
+
+        @pl.when(jnp.logical_not(first))
+        def _():
+            for c in range(2):
+                landed(u_near.at[3 - k, pl.ds(64 * c, 64), :], u_sem.at[1, k, c])
+            u_sum[...] += gram(split(u_near[3 - k]), split(u_chip[3 - k]), NT)
 
     def cross_v(k):
         landed(v_pair.at[1, k], v_sem.at[1, 2 + k])
@@ -208,19 +247,21 @@
         b = [v_pair[1, k], v_pair[1, 2 + k], v_fwd[k], v_pair[0, 2 + k]]
         return gram(split(jnp.concatenate(a, axis=0)), split(jnp.concatenate(b, axis=0)), TN)
 
+    pass_on(0)
+    told(0)
+    tell(1)
+    pass_on(1)
     near_u(0)
-    u_sum[...] = gram(split(u_chip[0]), split(u_near[0]), NT) + gram(split(u_near[3]), split(u_chip[3]), NT)
+    told(1)
+    tell(2)
     v_cross = cross_v(0)
     near_u(1)
-    u_sum[...] += gram(split(u_chip[1]), split(u_near[1]), NT)
-
-    @pl.when(jnp.logical_not(first_last))
-    def _():
-        u_sum[...] += gram(split(u_near[2]), split(u_chip[2]), NT)
-
-    @pl.when(last_first)
-    def _():
-        u_sum[...] += gram(split(u_chip[2]), split(u_extra[...]), NT)
+    @pl.when(second)
+    def _():
+        for k in range(2):
+            for c in range(2):
+                landed(u_extra.at[1 - k, pl.ds(64 * c, 64), :], extra_sem.at[k, c])
+            u_sum[...] += gram(split(u_extra[1 - k]), split(u_near[3 - k]), NT)
 
     row = lax.broadcasted_iota(jnp.int32, (128, 128), 0)
     col = lax.broadcasted_iota(jnp.int32, (128, 128), 1)
@@ -231,6 +272,8 @@
     tile[1:2] = lag_row(jnp.where(col < row, far, near))
     tile[2:3] = lag_row(jnp.where(col < row, near, far))
     told(2)
+    for load in lags:
+        load.wait()
 
     def all_sum(src, got, own, group, index):
         got[own] = src[...]
@@ -268,14 +311,13 @@
 
     for copy in sends:
         copy.wait_send()
-    for c in range(2):
-        @pl.when(jnp.logical_not(last_first))
+    for piece in pieces:
+        remote(*to_before(*piece)).wait_send()
+        remote(*to_after(*piece)).wait_send()
+
+        @pl.when(first)
         def _():
-            remote(*to_after(c, 1), base_slot + c).wait_send()
-
-        @pl.when(first_last)
-        def _():
-            remote(*to_close(c), base_slot + 2 + c).wait_send()
+            remote(*hand_on(*piece)).wait_send()
 
     landed(got1.at[pl.ds(0, 15)], red_send.at[0])
     landed(got2.at[pl.ds(0, 15)], red_send.at[1])
@@ -287,8 +329,8 @@
     block = (8, 64, 256)
     return pl.pallas_call(
         kernel,
-        out_shape=jax.ShapeDtypeStruct((3, 16), F32),
-        in_specs=[hbm] * 3 + [vmem] * 3,
+        out_shape=pltpu.VMEM((3, 16), F32),
+        in_specs=[hbm] * 6,
         out_specs=vmem,
         scratch_shapes=[
             pltpu.VMEM(block, F32),
@@ -296,7 +338,8 @@
             pltpu.VMEM(block, F32),
             pltpu.VMEM((4, 128, 256), F32),
             pltpu.VMEM((4, 128, 256), F32),
-            pltpu.VMEM((128, 256), F32),
+            pltpu.VMEM((2, 128, 256), F32),
+            pltpu.VMEM((2, 2, 64, 256), F32),
             pltpu.VMEM((128, 128), F32),
             pltpu.VMEM((2, 4, 64, 256), F32),
             pltpu.VMEM((4, 64, 256), F32),
@@ -305,15 +348,21 @@
             pltpu.VMEM((4, 128), F32),
             pltpu.VMEM((16, 4, 128), F32),
             pltpu.SemaphoreType.DMA((4,)),
-            pltpu.SemaphoreType.DMA((23,)),
+            pltpu.SemaphoreType.DMA((25,)),
             pltpu.SemaphoreType.DMA,
             pltpu.SemaphoreType.DMA((2, 2, 2)),
-            pltpu.SemaphoreType.DMA((2,)),
+            pltpu.SemaphoreType.DMA((2, 2)),
+            pltpu.SemaphoreType.DMA((2, 2)),
             pltpu.SemaphoreType.DMA((2, 4)),
             pltpu.SemaphoreType.DMA((2, 2)),
             pltpu.SemaphoreType.DMA((2,)),
             pltpu.SemaphoreType.DMA((2,)),
             pltpu.SemaphoreType.REGULAR((3,)),
+            pltpu.SemaphoreType.REGULAR,
+            pltpu.VMEM((1, 16), jnp.int32),
+            pltpu.VMEM((1, 16), jnp.int32),
+            pltpu.VMEM((1, 16), jnp.int32),
+            pltpu.SemaphoreType.DMA((3,)),
         ],
         compiler_params=pltpu.CompilerParams(collective_id=0, has_side_effects=True),
     )(u_field, v_field, w_field, sep_x.reshape(1, 16), sep_y.reshape(1, 16), sep_z.reshape(1, 16))

time: 37.8 us -> 33.3 us (0.88)
  Pallas kernels: 36.4 us -> 32.6 us
  local copies, waits for them, and re-layouts: 1.26 us -> 0.58 us
    pallas_call x1, Pallas kernels: 36.4 us -> 32.6 us  [local(): pl.pallas_call(kernel, out_shape=pltpu.VMEM((3, 16), F32), in_specs=[hbm]...]
    unnamed x1, local copies, waits for them, and re-layouts: 1.26 us -> 0.58 us
where the time goes in v3:
time: 33.3 us; the launch traced here: 33.2 us
  Pallas kernels  32.6 us (98%)
  local copies, waits for them, and re-layouts  0.58 us (2%)
    pallas_call x1, Pallas kernels, local(): pl.pallas_call(kernel, out_shape=pltpu.VMEM((3, 16), F32), in_specs=[hbm]...  32.6 us

profile of v3, /device:TPU:1, one launch (start us, length us, event | category | flops | bytes accessed | tf_op | source)
XLA Modules:
  0.0 33.2 jit_solution(10012313657572357768)
XLA Ops:
  0.0 32.6 %shard_map.64 = f32[3,16]{1,0:T(4,128)S(1)} custom-call(f32[8,64,256]{2,1,0:T(8,128)} %u_hbm.1, f32[8,64,256]{2,1,0:T(8,128)} %v_hbm.1, f32[8,64,256]{2,1,0:T(8,128)} %w_hbm.1, s32[1,16]{1,0:T(1,128)} %bitcast.3, s32[1,16]{1,0:T(1,128)} %bitcast.4, s32[1,16]{1,0:T(1,128)} %bitcast.5), custom_call_target="tpu_custom_call" | custom-call | tf_op jit(solution)/shard_map/pallas_call | solution.py:330
  32.6 0.6 %copy.8 = f32[3,16]{1,0:T(4,128)} copy(f32[3,16]{1,0:T(4,128)S(1)} %shard_map.64) | data formatting | bytes 384

commit v4 on v3

--- a/solution.py
+++ b/solution.py
@@ -41,7 +41,7 @@
 
 def kernel(u_hbm, v_hbm, w_hbm, sx_hbm, sy_hbm, sz_hbm, out_ref,
            u_own, v_own, w_own, u_chip, u_near, u_extra, u_hand, u_sum, v_pair, v_fwd, tile, got1, mid, got2,
-           load_sem, send_sem, d2d_sem, u_sem, extra_sem, hand_sem, v_sem, y_sem, red_send, red_recv, token, back, sx_ref, sy_ref, sz_ref, sep_sem):
+           load_sem, send_sem, d2d_sem, u_sem, extra_sem, hand_sem, v_sem, y_sem, red_send, red_recv, token, back, wrap_back, sx_ref, sy_ref, sz_ref, sep_sem):
     gy = lax.axis_index("gy")
     gx = lax.axis_index("gx")
     y, x_hi = gy // 2, gy % 2
@@ -147,6 +147,14 @@
     def to_second(k, c):
         return (u_own.at[4 * c + 3 - k], u_extra.at[1 - k, rows, :], extra_sem.at[k, core], two_on[c], 17 + 2 * k + c)
 
+    @pl.when(jnp.logical_not(first))
+    def _():
+        signal(back, chip_before)
+
+    @pl.when(last)
+    def _():
+        signal(wrap_back, wrapped)
+
     loads[1].wait()
 
     @pl.when(first)
@@ -158,13 +166,11 @@
     def _():
         for piece in pieces:
             remote(*to_before(*piece)).start()
-        signal(back, chip_before)
 
     @pl.when(last)
     def _():
         for piece in pieces:
             remote(*to_second(*piece)).start()
-        signal(back, wrapped)
 
     loads[0].wait()
     for j in range(4):
@@ -195,17 +201,21 @@
 
     @pl.when(jnp.logical_not(last))
     def _():
-        pl.semaphore_wait(back, 2 + 2 * (1 - jnp.minimum(z, 1)))
+        pl.semaphore_wait(back, 2)
         for piece in pieces:
             remote(*to_after(*piece)).start()
+
+    @pl.when(first)
+    def _():
+        pl.semaphore_wait(wrap_back, 2)
+
+    tell(0)
 
     @pl.when(first)
     def _():
         for k, c in pieces:
             landed(u_hand.at[k, c], hand_sem.at[k, c])
             remote(*hand_on(k, c)).start()
-
-    tell(0)
 
     v_split = split(v_own[...].reshape(512, 256))
     v_same = gram(v_split, v_split, TN)
@@ -359,6 +369,7 @@
             pltpu.SemaphoreType.DMA((2,)),
             pltpu.SemaphoreType.REGULAR((3,)),
             pltpu.SemaphoreType.REGULAR,
+            pltpu.SemaphoreType.REGULAR,
             pltpu.VMEM((1, 16), jnp.int32),
             pltpu.VMEM((1, 16), jnp.int32),
             pltpu.VMEM((1, 16), jnp.int32),

time: 33.3 us -> 29.9 us (0.90)
  Pallas kernels: 32.6 us -> 29.2 us
    pallas_call x1, Pallas kernels: 32.6 us -> 29.2 us  [local(): pl.pallas_call(kernel, out_shape=pltpu.VMEM((3, 16), F32), in_specs=[hbm]...]
where the time goes in v4:
time: 29.9 us; the launch traced here: 29.8 us
  Pallas kernels  29.2 us (98%)
  local copies, waits for them, and re-layouts  0.58 us (2%)
    pallas_call x1, Pallas kernels, local(): pl.pallas_call(kernel, out_shape=pltpu.VMEM((3, 16), F32), in_specs=[hbm]...  29.2 us

profile of v4, /device:TPU:1, one launch (start us, length us, event | category | flops | bytes accessed | tf_op | source)
XLA Modules:
  0.0 29.8 jit_solution(5326837022963546130)
XLA Ops:
  0.0 29.2 %shard_map.64 = f32[3,16]{1,0:T(4,128)S(1)} custom-call(f32[8,64,256]{2,1,0:T(8,128)} %u_hbm.1, f32[8,64,256]{2,1,0:T(8,128)} %v_hbm.1, f32[8,64,256]{2,1,0:T(8,128)} %w_hbm.1, s32[1,16]{1,0:T(1,128)} %bitcast.3, s32[1,16]{1,0:T(1,128)} %bitcast.4, s32[1,16]{1,0:T(1,128)} %bitcast.5), custom_call_target="tpu_custom_call" | custom-call | tf_op jit(solution)/shard_map/pallas_call | solution.py:340
  29.2 0.6 %copy.8 = f32[3,16]{1,0:T(4,128)} copy(f32[3,16]{1,0:T(4,128)S(1)} %shard_map.64) | data formatting | bytes 384
